TPU v7x, 32 devices: a whole 2x2x4 slice. The times are simulated.
32 devices in a mesh: gx: 2 (over x), gy: 4 (over y, core), gz: 4 (over z).
Axes of the slice: x: 2, y: 2, z: 4, core: 2. Of those that a mesh axis runs over, the one named last changes fastest.
Arguments:
- flow_pops: float32 [19, 16, 32, 512], P(None, 'gx', 'gy', 'gz'), may hold values from 0 to 0.6, as said below
- heat_pops: float32 [7, 16, 32, 512], P(None, 'gx', 'gy', 'gz'), may hold values from -0.2 to 0.2
Outputs:
- flow_out: float32 [19, 16, 32, 512], P(None, 'gx', 'gy', 'gz')
- heat_out: float32 [7, 16, 32, 512], P(None, 'gx', 'gy', 'gz')
- nusselt: float32 [], replicated
Inputs may be any that keep to these rules, and one draw needn't show every extreme that they name: `flow_pops`: positive flow populations.
All inputs are finite; a program needn't handle non-finite values.
Results may differ from a plain program's by a relative error of at most 0.0001.
Values sent between devices are 32-bit elements; how exact they have to be, the bound alone decides.
A program may use at most 64 MiB of HBM per device.

v0:
```python
import functools

import jax
import jax.numpy as jnp
import numpy as np
from jax import lax
from jax.experimental import pallas as pl
from jax.experimental.pallas import tpu as pltpu
from jax.sharding import PartitionSpec as P

STEPS = 3

FLOW_SET = np.array(
    [
        [0, 0, 0],
        [1, 0, 0],
        [-1, 0, 0],
        [0, 1, 0],
        [0, -1, 0],
        [0, 0, 1],
        [0, 0, -1],
        [1, 1, 0],
        [-1, -1, 0],
        [1, -1, 0],
        [-1, 1, 0],
        [1, 0, 1],
        [-1, 0, -1],
        [1, 0, -1],
        [-1, 0, 1],
        [0, 1, 1],
        [0, -1, -1],
        [0, 1, -1],
        [0, -1, 1],
    ]
)
FLOW_WEIGHT = np.array([1.0 / 3.0] + [1.0 / 18.0] * 6 + [1.0 / 36.0] * 12)
HEAT_WEIGHT = np.array([0.25] + [0.125] * 6)
LATTICE = [tuple(int(c) for c in v) for v in np.concatenate([FLOW_SET, FLOW_SET[:7]], axis=0)]
WEIGHTS = [float(w) for w in np.concatenate([FLOW_WEIGHT, HEAT_WEIGHT])]
OPPOSITE = (
    [0]
    + [q + 1 if q % 2 else q - 1 for q in range(1, 19)]
    + [19]
    + [q - 1 if q % 2 else q + 1 for q in range(20, 26)]
)
TAU_FLOW = 0.6
TAU_HEAT = 0.7
GRAVITY_LIFT = 0.01
HOT_WALL = 0.5
COLD_WALL = -0.5
DIFFUSIVITY = (TAU_HEAT - 0.5) / 4.0

MEMBERS = {
    (axis, sign): [q for q in range(26) if LATTICE[q][axis] == sign]
    for axis in range(3)
    for sign in (1, -1)
}
FACE = len(MEMBERS[0, 1])
STORED = (
    MEMBERS[0, 1] + MEMBERS[0, -1] + [q for q in range(26) if LATTICE[q][0] == 0]
)
SLOT = [STORED.index(q) for q in range(26)]
SIDES = (1, -1)
UNROLL = 3
LINKS = sorted({v for v in LATTICE if v != (0, 0, 0)})


def side(sign):
    return 0 if sign == 1 else 1


def moments(f, g):
    rho = functools.reduce(lambda a, b: a + b, f)
    warmth = functools.reduce(lambda a, b: a + b, g)
    flow = []
    for axis in range(3):
        total = None
        for q in range(1, 19, 2):
            if LATTICE[q][axis]:
                odd = f[q] - f[q + 1]
                if total is None:
                    total = odd
                else:
                    total = total + odd if LATTICE[q][axis] == 1 else total - odd
        flow.append(total)
    push = GRAVITY_LIFT * rho * warmth
    inv = 1.0 / rho
    return (rho, warmth, push, flow[0] * inv, flow[1] * inv, (flow[2] + 0.5 * push) * inv)


def collide(f, g):
    rho, warmth, push, ux, uy, uz = moments(f, g)
    rate = 1.0 / TAU_FLOW
    lift = 1.0 - 0.5 / TAU_FLOW
    keep = 1.0 - rate
    base = (rate * rho) * (1.0 - 1.5 * (ux * ux + uy * uy + uz * uz)) - (3.0 * lift) * uz * push
    quad = (4.5 * rate) * rho
    line = (3.0 * rate) * rho
    push3 = (3.0 * lift) * push
    push9 = (9.0 * lift) * push
    post = [None] * 26
    post[0] = keep * f[0] + WEIGHTS[0] * base
    u = (ux, uy, uz)
    for q in range(1, 19, 2):
        c = LATTICE[q]
        along = None
        for axis in range(3):
            if c[axis]:
                if along is None:
                    along = u[axis]
                else:
                    along = along + u[axis] if c[axis] == 1 else along - u[axis]
        inner = quad * along
        odd = line * along
        if c[2] == 1:
            inner, odd = inner + push9, odd + push3
        elif c[2] == -1:
            inner, odd = inner - push9, odd - push3
        even = WEIGHTS[q] * (base + along * inner)
        odd = WEIGHTS[q] * odd
        post[q] = keep * f[q] + (even + odd)
        post[q + 1] = keep * f[q + 1] + (even - odd)
    heat_rate = 1.0 / TAU_HEAT
    heat_keep = 1.0 - heat_rate
    post[19] = heat_keep * g[0] + (WEIGHTS[19] * heat_rate) * warmth
    still = (WEIGHTS[20] * heat_rate) * warmth
    for axis in range(3):
        drift = (4.0 * WEIGHTS[20] * heat_rate) * warmth * u[axis]
        q = 20 + 2 * axis
        post[q] = heat_keep * g[q - 19] + (still + drift)
        post[q + 1] = heat_keep * g[q - 18] + (still - drift)
    return post


def kernel(
    sizes, flow_in, heat_in, flow_out, heat_out, nusselt,
    cur, post, sy, ry, sz, rz, syz, ryz, sums,
    in_sem, send_sem, recv_sem, sum_send, sum_recv,
):
    count_x, count_y, count_z = sizes
    nx, ny, nz = cur.shape[1:]
    gx, gy, gz = (lax.axis_index(a) for a in ("gx", "gy", "gz"))
    has = {1: gz < count_z - 1, -1: gz > 0}
    everyone = count_x * count_y * count_z
    me = (gx * count_y + gy) * count_z + gz

    def device(v):
        return {
            "gx": lax.rem(gx + v[0] + count_x, count_x),
            "gy": lax.rem(gy + v[1] + count_y, count_y),
            "gz": gz + v[2],
        }

    def ahead(distance):
        other = lax.rem(me + distance, everyone)
        row = other // count_z
        return {"gx": row // count_y, "gy": lax.rem(row, count_y), "gz": lax.rem(other, count_z)}

    def load(x):
        return (
            pltpu.make_async_copy(flow_in.at[:, x], cur.at[0:19, x], in_sem.at[0, x]),
            pltpu.make_async_copy(heat_in.at[:, x], cur.at[19:26, x], in_sem.at[1, x]),
        )

    for x in [0, nx - 1] + list(range(1, nx - 1)):
        for copy in load(x):
            copy.start()

    barrier = pltpu.get_barrier_semaphore()
    near = sorted({(v[0] % count_x, v[1] % count_y, v[2]) for v in LINKS})
    reach = (count_x // 2, count_y // 2, count_z - 1)
    joined = max(reach) <= STEPS and sum(reach) <= 2 * STEPS
    if joined:
        for v in near:
            if v[2] == 0:
                pl.semaphore_signal(barrier, inc=1, device_id=device(v))
        for sign in SIDES:
            @pl.when(has[sign])
            def _():
                for v in near:
                    if v[2] == sign:
                        pl.semaphore_signal(barrier, inc=1, device_id=device(v))
    else:
        @pl.loop(1, everyone)
        def _(d):
            pl.semaphore_signal(barrier, inc=1, device_id=ahead(d))

    def greet():
        if joined:
            count = len([v for v in near if v[2] == 0])
            for sign in SIDES:
                count += jnp.where(has[sign], len([v for v in near if v[2] == sign]), 0)
        else:
            count = everyone - 1
        pl.semaphore_wait(barrier, count)

    lane = lax.broadcasted_iota(jnp.int32, (ny, nz), 1)
    row = lax.broadcasted_iota(jnp.int32, (ny, nz), 0)
    first_row, last_row = row == 0, row == ny - 1
    first_lane, last_lane = lane == 0, lane == nz - 1

    def message(s, v):
        i = LINKS.index(v)
        x, y, z = v
        if z == 0:
            start = 0 if x == 1 else FACE
            edge, halo = (nx, 0) if x == 1 else (1, nx + 1)
            if y == 0:
                src = post.at[s, start : start + FACE, edge]
                dst = post.at[s, start : start + FACE, halo]
            elif x == 0:
                src = sy.at[s, side(y), :, 1 : nx + 1]
                dst = ry.at[s, side(y), :, 1 : nx + 1]
            else:
                j = MEMBERS[1, y].index(LATTICE.index(v))
                src = sy.at[s, side(y), j, edge]
                dst = ry.at[s, side(y), j, halo]
        elif y == 0:
            src = sz.at[s, side(z), 0 if x == 0 else 1]
            dst = rz.at[s, side(z), 0 if x == 0 else 1 + side(x)]
        else:
            src = syz.at[s, side(z), side(y)]
            dst = ryz.at[s, side(z), side(y)]
        return pltpu.make_async_remote_copy(
            src_ref=src, dst_ref=dst, send_sem=send_sem.at[s, i], recv_sem=recv_sem.at[s, i],
            device_id=device(v),
        )

    def send(s, links):
        for sign in SIDES:
            @pl.when(has[sign])
            def _():
                for v in links:
                    if v[2] == sign:
                        message(s, v).start()
        for v in links:
            if v[2] == 0:
                message(s, v).start()

    def receive(s):
        for v in LINKS:
            if v[2] == 0:
                message(s, v).wait_recv()
        for sign in SIDES:
            @pl.when(has[-sign])
            def _():
                for v in LINKS:
                    if v[2] == sign:
                        message(s, v).wait_recv()

    hops = lambda v: -sum(abs(c) for c in v)
    early = sorted([v for v in LINKS if v[0]], key=hops)
    late = sorted([v for v in LINKS if not v[0]], key=hops)
    width = FACE

    def keep_plane(s, x, values, packs):
        for q in range(26):
            post[s, SLOT[q], x + 1] = values[q]
        for sign in SIDES:
            r = ny - 1 if sign == 1 else 0
            for j, q in enumerate(MEMBERS[1, sign]):
                sy[s, side(sign), j, x + 1] = values[q][r : r + 1, :]
        new = []
        for sign, pack in zip(SIDES, packs):
            source = nz - 1 if sign == 1 else 0
            part = None
            for j, q in enumerate(MEMBERS[2, sign]):
                turned = pltpu.roll(values[q], (j - source) % nz, 1)
                part = turned if part is None else jnp.where(lane == j, turned, part)
            base = (x + 1) * width
            part = pltpu.roll(part, base, 1)
            new.append(jnp.where((lane >= base) & (lane < base + width), part, pack))
        return tuple(new)

    def run_planes(s, body):
        zero = jnp.zeros((ny, nz), jnp.float32)
        packs = lax.fori_loop(
            0, 2, lambda i, p: keep_plane(s, i * (nx - 1), body(i * (nx - 1)), p), (zero, zero), unroll=True
        )
        return packs

    def advance(s, body, before_send):
        packs = run_planes(s, body)
        for sign, pack in zip(SIDES, packs):
            sz[s, side(sign), 1] = pack
        before_send()
        send(s, early)
        packs = lax.fori_loop(
            1, nx - 1, lambda x, p: keep_plane(s, x, body(x), p), packs, unroll=UNROLL
        )
        for sign, pack in zip(SIDES, packs):
            sz[s, side(sign), 0] = pack
            for sign_y in SIDES:
                r = ny - 1 if sign_y == 1 else 0
                syz[s, side(sign), side(sign_y)] = pack[r : r + 1, :]
        send(s, late)

    def columns(s):
        result = {}
        for sign in SIDES:
            straight = rz[s, side(sign), 0]
            low = pltpu.roll(rz[s, side(sign), 1], (-nx * width) % nz, 1)
            high = pltpu.roll(rz[s, side(sign), 2], (nx * width) % nz, 1)
            result[sign, 0] = jnp.where(
                lane < width, low, jnp.where(lane >= (nx + 1) * width, high, straight)
            )
            for sign_y in SIDES:
                turned = pltpu.roll(straight, sign_y % ny, 0)
                edge = jnp.broadcast_to(ryz[s, side(sign), side(sign_y)], (ny, nz))
                result[sign, sign_y] = jnp.where(
                    first_row if sign_y == 1 else last_row, edge, turned
                )
        return result

    def pull(s, x, beyond, q):
        cx, cy, cz = LATTICE[q]
        at = x - cx + 1
        value = post[s, SLOT[q], at]
        if cy:
            j = MEMBERS[1, cy].index(q)
            edge = jnp.broadcast_to(ry[s, side(cy), j, at], (ny, nz))
            value = jnp.where(
                first_row if cy == 1 else last_row, edge, pltpu.roll(value, cy % ny, 0)
            )
        if cz:
            j = MEMBERS[2, cz].index(q)
            target = 0 if cz == 1 else nz - 1
            outer = pltpu.roll(beyond[cz, cy], lax.rem(target - (at * width + j) + nz, nz), 1)
            back = post[s, SLOT[OPPOSITE[q]], x + 1]
            if q >= 19:
                back = 2.0 * WEIGHTS[q] * (HOT_WALL if cz == 1 else COLD_WALL) - back
            outer = jnp.where(has[-cz], outer, back)
            value = jnp.where(
                first_lane if cz == 1 else last_lane, outer, pltpu.roll(value, cz % nz, 1)
            )
        return value

    def fresh(x):
        for copy in load(x):
            copy.wait()
        return collide([cur[q, x] for q in range(19)], [cur[q, x] for q in range(19, 26)])

    advance(0, fresh, greet)

    def step(s, carry):
        receive(s)
        beyond = columns(s)

        def body(x):
            values = [pull(s, x, beyond, q) for q in range(26)]
            return collide(values[:19], values[19:])

        advance(s + 1, body, lambda: None)
        return carry

    lax.fori_loop(0, STEPS - 1, step, 0)

    last = STEPS - 1
    receive(last)
    beyond = columns(last)

    def finish(x, total):
        values = [pull(last, x, beyond, q) for q in range(26)]
        for q in range(19):
            flow_out[q, x] = values[q]
        for q in range(7):
            heat_out[q, x] = values[19 + q]
        _, warmth, _, _, _, uz = moments(values[:19], values[19:])
        return total + uz * warmth

    total = lax.fori_loop(0, nx, finish, jnp.zeros((ny, nz), jnp.float32), unroll=4)
    sums[me] = jnp.sum(total, axis=0, keepdims=True)

    def send_sum(target):
        pltpu.make_async_remote_copy(
            src_ref=sums.at[me], dst_ref=sums.at[me],
            send_sem=sum_send, recv_sem=sum_recv, device_id=target,
        ).start()

    if joined:
        xs, ys, zs = (
            [lax.rem(at + d, n) for d in range(n)] for at, n in zip((gx, gy, gz), sizes)
        )
        for dz in reversed(range(count_z)):
            for dx in reversed(range(count_x)):
                for dy in reversed(range(count_y)):
                    if dx or dy or dz:
                        send_sum({"gx": xs[dx], "gy": ys[dy], "gz": zs[dz]})
    else:
        pl.loop(1, everyone)(lambda d: send_sum(ahead(d)))

    for s in range(STEPS):
        for v in LINKS:
            if v[2] == 0:
                message(s, v).wait_send()
        for sign in SIDES:
            @pl.when(has[sign])
            def _():
                for v in LINKS:
                    if v[2] == sign:
                        message(s, v).wait_send()
    all_rows = pltpu.make_async_remote_copy(
        src_ref=sums.at[pl.ds(0, everyone - 1)], dst_ref=sums.at[pl.ds(0, everyone - 1)],
        send_sem=sum_send, recv_sem=sum_recv, device_id=ahead(1),
    )
    all_rows.wait_send()
    all_rows.wait_recv()
    cells = nx * ny * nz * count_x * count_y * count_z
    scale = nz * count_z / (DIFFUSIVITY * (HOT_WALL - COLD_WALL)) / cells
    nusselt[0, 0] = 1.0 + scale * jnp.sum(jnp.sum(sums[...], axis=0))


def write_out(flow, heat, flow_out, heat_out, sem):
    copies = (
        pltpu.make_async_copy(flow, flow_out, sem.at[0]),
        pltpu.make_async_copy(heat, heat_out, sem.at[1]),
    )
    for copy in copies:
        copy.start()
    for copy in copies:
        copy.wait()


def per_device(sizes, flow_pops, heat_pops):
    nx, ny, nz = flow_pops.shape[1:]
    count_x, count_y, count_z = sizes
    f32 = jnp.float32
    dma = pltpu.SemaphoreType.DMA
    hbm = pl.BlockSpec(memory_space=pltpu.HBM)
    vmem = pl.BlockSpec(memory_space=pltpu.VMEM)
    flow, heat, nusselt = pl.pallas_call(
        functools.partial(kernel, sizes),
        out_shape=(
            jax.ShapeDtypeStruct(flow_pops.shape, f32),
            jax.ShapeDtypeStruct(heat_pops.shape, f32),
            jax.ShapeDtypeStruct((1, 1), f32),
        ),
        in_specs=[hbm, hbm],
        out_specs=(vmem, vmem, pl.BlockSpec(memory_space=pltpu.SMEM)),
        scratch_shapes=[
            pltpu.VMEM((26, nx, ny, nz), f32),
            pltpu.VMEM((STEPS, 26, nx + 2, ny, nz), f32),
            pltpu.VMEM((STEPS, 2, FACE, nx + 2, 1, nz), f32),
            pltpu.VMEM((STEPS, 2, FACE, nx + 2, 1, nz), f32),
            pltpu.VMEM((STEPS, 2, 2, ny, nz), f32),
            pltpu.VMEM((STEPS, 2, 3, ny, nz), f32),
            pltpu.VMEM((STEPS, 2, 2, 1, nz), f32),
            pltpu.VMEM((STEPS, 2, 2, 1, nz), f32),
            pltpu.VMEM((count_x * count_y * count_z, 1, nz), f32),
            dma((2, nx)),
            dma((STEPS, len(LINKS))),
            dma((STEPS, len(LINKS))),
            dma,
            dma,
        ],
        compiler_params=pltpu.CompilerParams(
            collective_id=0, has_side_effects=True, vmem_limit_bytes=55_000_000
        ),
    )(flow_pops, heat_pops)
    flow, heat = pl.pallas_call(
        write_out,
        out_shape=(
            jax.ShapeDtypeStruct(flow_pops.shape, f32),
            jax.ShapeDtypeStruct(heat_pops.shape, f32),
        ),
        in_specs=[vmem, vmem],
        out_specs=(hbm, hbm),
        scratch_shapes=[dma((2,))],
        compiler_params=pltpu.CompilerParams(vmem_limit_bytes=1024 * 1024),
    )(flow, heat)
    return flow, heat, nusselt.reshape(())


def solution(mesh):
    placed = P(None, "gx", "gy", "gz")
    sizes = tuple(mesh.shape[a] for a in ("gx", "gy", "gz"))
    return jax.shard_map(
        functools.partial(per_device, sizes),
        mesh=mesh,
        in_specs=(placed, placed),
        out_specs=(placed, placed, P()),
        check_vma=False,
    )
```

profile of v0, /device:TPU:0, one launch (start us, length us, event | category | flops | bytes accessed | tf_op | source)
XLA Modules:
  0.0 27.8 jit_solution(13706903612295605228)
XLA Ops:
  0.6 0.0 copy-start
  0.6 0.9 %copy-done = f32[7,8,8,128]{3,2,1,0:T(8,128)S(1)} copy-done((f32[7,8,8,128]{3,2,1,0:T(8,128)S(1)}, f32[7,8,8,128]{3,2,1,0:T(8,128)}, u32[]{:S(2)}) %copy-start) | copy-done | bytes 229400
  1.6 23.5 %shard_map.49 = (f32[19,8,8,128]{3,2,1,0:T(8,128)S(1)}, f32[7,8,8,128]{3,2,1,0:T(8,128)S(1)}, f32[1,1]{1,0:T(1,128)}) custom-call(f32[19,8,8,128]{3,2,1,0:T(8,128)} %flow_in.1, f32[7,8,8,128]{3,2,1,0:T(8,128)S(1)} %copy-done), custom_call_target="tpu_custom_call" | custom-call | tf_op jit(solution)/shard_map/pallas_call | solution.py:431
  25.1 0.9 %shard_map.50 = (f32[19,8,8,128]{3,2,1,0:T(8,128)}, f32[7,8,8,128]{3,2,1,0:T(8,128)}) custom-call(f32[19,8,8,128]{3,2,1,0:T(8,128)S(1)} %get-tuple-element.8.flow, f32[7,8,8,128]{3,2,1,0:T(8,128)S(1)} %get-tuple-element.9.heat), custom_call_target="tpu_custom_call" | custom-call | tf_op jit(solution)/shard_map/pallas_call | solution.py:460
Async XLA Ops:
  0.6 0.9 %copy-start = (f32[7,8,8,128]{3,2,1,0:T(8,128)S(1)}, f32[7,8,8,128]{3,2,1,0:T(8,128)}, u32[]{:S(2)}) copy-start(f32[7,8,8,128]{3,2,1,0:T(8,128)} %heat_in.1) | copy-start | bytes 688132
where the time goes:
time: 28 us; the launch traced here: 27.8 us
  Pallas kernels  24.5 us (88%)
  between operations  2.41 us (9%)
  local copies, waits for them, and re-layouts  0.93 us (3%)
    pallas_call x1, Pallas kernels, per_device(): pl.pallas_call(functools.partial(kernel, sizes), out_shape=(jax.ShapeDtyp...  23.5 us
    unnamed x2, local copies, waits for them, and re-layouts  0.93 us
    pallas_call x1, Pallas kernels, per_device(): pl.pallas_call(write_out, out_shape=(jax.ShapeDtypeStruct(flow_pops.shape...  0.91 us

commit v1 on v0

--- a/solution.py
+++ b/solution.py
@@ -133,7 +133,7 @@
 
 
 def kernel(
-    sizes, flow_in, heat_in, flow_out, heat_out, nusselt,
+    sizes, flow_in, heat_in, result,
     cur, post, sy, ry, sz, rz, syz, ryz, sums,
     in_sem, send_sem, recv_sem, sum_send, sum_recv,
 ):
@@ -362,9 +362,9 @@
     def finish(x, total):
         values = [pull(last, x, beyond, q) for q in range(26)]
         for q in range(19):
-            flow_out[q, x] = values[q]
+            result[q, x] = values[q]
         for q in range(7):
-            heat_out[q, x] = values[19 + q]
+            result[19 + q, x] = values[19 + q]
         _, warmth, _, _, _, uz = moments(values[:19], values[19:])
         return total + uz * warmth
 
@@ -407,14 +407,19 @@
     all_rows.wait_recv()
     cells = nx * ny * nz * count_x * count_y * count_z
     scale = nz * count_z / (DIFFUSIVITY * (HOT_WALL - COLD_WALL)) / cells
-    nusselt[0, 0] = 1.0 + scale * jnp.sum(jnp.sum(sums[...], axis=0))
-
-
-def write_out(flow, heat, flow_out, heat_out, sem):
-    copies = (
-        pltpu.make_async_copy(flow, flow_out, sem.at[0]),
-        pltpu.make_async_copy(heat, heat_out, sem.at[1]),
-    )
+    result[26, 0, 0:1, :] = jnp.full((1, nz), 1.0 + scale * jnp.sum(jnp.sum(sums[...], axis=0)))
+
+
+def write_out(result, flow_out, heat_out, nusselt_out, small, sem):
+    small[...] = result[26, 0, 0:1, 0:1]
+    copies = []
+    for q in range(0, 19, 2):
+        n = min(2, 19 - q)
+        copies.append(pltpu.make_async_copy(result.at[q : q + n], flow_out.at[q : q + n], sem.at[q]))
+    for q in range(0, 7, 2):
+        n = min(2, 7 - q)
+        copies.append(pltpu.make_async_copy(result.at[19 + q : 19 + q + n], heat_out.at[q : q + n], sem.at[19 + q]))
+    copies.append(pltpu.make_async_copy(small, nusselt_out, sem.at[26]))
     for copy in copies:
         copy.start()
     for copy in copies:
@@ -428,15 +433,11 @@
     dma = pltpu.SemaphoreType.DMA
     hbm = pl.BlockSpec(memory_space=pltpu.HBM)
     vmem = pl.BlockSpec(memory_space=pltpu.VMEM)
-    flow, heat, nusselt = pl.pallas_call(
+    result = pl.pallas_call(
         functools.partial(kernel, sizes),
-        out_shape=(
-            jax.ShapeDtypeStruct(flow_pops.shape, f32),
-            jax.ShapeDtypeStruct(heat_pops.shape, f32),
-            jax.ShapeDtypeStruct((1, 1), f32),
-        ),
+        out_shape=pltpu.VMEM((27, nx, ny, nz), f32),
         in_specs=[hbm, hbm],
-        out_specs=(vmem, vmem, pl.BlockSpec(memory_space=pltpu.SMEM)),
+        out_specs=vmem,
         scratch_shapes=[
             pltpu.VMEM((26, nx, ny, nz), f32),
             pltpu.VMEM((STEPS, 26, nx + 2, ny, nz), f32),
@@ -454,20 +455,21 @@
             dma,
         ],
         compiler_params=pltpu.CompilerParams(
-            collective_id=0, has_side_effects=True, vmem_limit_bytes=55_000_000
+            collective_id=0, has_side_effects=True, vmem_limit_bytes=55000000
         ),
-    )(flow_pops, heat_pops)
-    flow, heat = pl.pallas_call(
+    )(pltpu.with_memory_space_constraint(flow_pops, pltpu.HBM), pltpu.with_memory_space_constraint(heat_pops, pltpu.HBM))
+    flow, heat, nusselt = pl.pallas_call(
         write_out,
         out_shape=(
             jax.ShapeDtypeStruct(flow_pops.shape, f32),
             jax.ShapeDtypeStruct(heat_pops.shape, f32),
+            jax.ShapeDtypeStruct((1, 1), f32),
         ),
-        in_specs=[vmem, vmem],
-        out_specs=(hbm, hbm),
-        scratch_shapes=[dma((2,))],
+        in_specs=[vmem],
+        out_specs=(hbm, hbm, hbm),
+        scratch_shapes=[pltpu.VMEM((1, 1), f32), dma((27,))],
         compiler_params=pltpu.CompilerParams(vmem_limit_bytes=1024 * 1024),
-    )(flow, heat)
+    )(result)
     return flow, heat, nusselt.reshape(())
 
 

time: 28 us -> 24.9 us (0.89)
  between operations: 2.41 us -> 0.64 us
  local copies, waits for them, and re-layouts: 0.93 us -> 0 us
  Pallas kernels: 24.5 us -> 24.2 us
    unnamed x2 -> x0, local copies, waits for them, and re-layouts: 0.93 us -> none
    pallas_call x1, Pallas kernels: 23.5 us -> 23 us  [per_device(): pl.pallas_call(functools.partial(kernel, sizes), out_shape=pltpu.VMEM((27...]
where the time goes in v1:
time: 24.9 us; the launch traced here: 24.8 us
  Pallas kernels  24.2 us (97%)
  between operations  0.64 us (3%)
    pallas_call x1, Pallas kernels, per_device(): pl.pallas_call(functools.partial(kernel, sizes), out_shape=pltpu.VMEM((27...  23 us
    pallas_call x1, Pallas kernels, per_device(): pl.pallas_call(write_out, out_shape=(jax.ShapeDtypeStruct(flow_pops.shape...  1.12 us

profile of v1, /device:TPU:0, one launch (start us, length us, event | category | flops | bytes accessed | tf_op | source)
XLA Modules:
  0.0 24.8 jit_solution(9916229116547524931)
XLA Ops:
  0.6 23.0 %shard_map.49.result = f32[27,8,8,128]{3,2,1,0:T(8,128)S(1)} custom-call(f32[19,8,8,128]{3,2,1,0:T(8,128)} %flow_in.1, f32[7,8,8,128]{3,2,1,0:T(8,128)} %heat_in.1), custom_call_target="tpu_custom_call" | custom-call | tf_op jit(solution)/shard_map/pallas_call | solution.py:436
  23.7 1.1 %shard_map.50 = (f32[19,8,8,128]{3,2,1,0:T(8,128)}, f32[7,8,8,128]{3,2,1,0:T(8,128)}, f32[1,1]{1,0:T(1,128)}) custom-call(f32[27,8,8,128]{3,2,1,0:T(8,128)S(1)} %shard_map.49.result), custom_call_target="tpu_custom_call" | custom-call | tf_op jit(solution)/shard_map/pallas_call | solution.py:461

commit v2 on v1

v2 whole, which is shorter than its diff:
```python
import functools

import jax
import jax.numpy as jnp
import numpy as np
from jax import lax
from jax.experimental import pallas as pl
from jax.experimental.pallas import tpu as pltpu
from jax.sharding import PartitionSpec as P

STEPS = 3

FLOW_SET = np.array(
    [
        [0, 0, 0],
        [1, 0, 0],
        [-1, 0, 0],
        [0, 1, 0],
        [0, -1, 0],
        [0, 0, 1],
        [0, 0, -1],
        [1, 1, 0],
        [-1, -1, 0],
        [1, -1, 0],
        [-1, 1, 0],
        [1, 0, 1],
        [-1, 0, -1],
        [1, 0, -1],
        [-1, 0, 1],
        [0, 1, 1],
        [0, -1, -1],
        [0, 1, -1],
        [0, -1, 1],
    ]
)
FLOW_WEIGHT = np.array([1.0 / 3.0] + [1.0 / 18.0] * 6 + [1.0 / 36.0] * 12)
HEAT_WEIGHT = np.array([0.25] + [0.125] * 6)
LATTICE = [tuple(int(c) for c in v) for v in np.concatenate([FLOW_SET, FLOW_SET[:7]], axis=0)]
WEIGHTS = [float(w) for w in np.concatenate([FLOW_WEIGHT, HEAT_WEIGHT])]
OPPOSITE = (
    [0]
    + [q + 1 if q % 2 else q - 1 for q in range(1, 19)]
    + [19]
    + [q - 1 if q % 2 else q + 1 for q in range(20, 26)]
)
TAU_FLOW = 0.6
TAU_HEAT = 0.7
GRAVITY_LIFT = 0.01
HOT_WALL = 0.5
COLD_WALL = -0.5
DIFFUSIVITY = (TAU_HEAT - 0.5) / 4.0
KEEP_FLOW = 1.0 - 1.0 / TAU_FLOW
KEEP_HEAT = 1.0 - 1.0 / TAU_HEAT

MEMBERS = {
    (axis, sign): [q for q in range(26) if LATTICE[q][axis] == sign]
    for axis in range(3)
    for sign in (1, -1)
}
FACE = len(MEMBERS[0, 1])
STORED = (
    MEMBERS[0, 1] + MEMBERS[0, -1] + [q for q in range(26) if LATTICE[q][0] == 0]
)
SLOT = [STORED.index(q) for q in range(26)]
SIDES = (1, -1)
UNROLL = True
LINKS = sorted({v for v in LATTICE if v != (0, 0, 0)})


EARLY = sorted([v for v in LINKS if v[0]], key=lambda v: sum(abs(c) for c in v))
LATE = sorted([v for v in LINKS if not v[0]], key=lambda v: -sum(abs(c) for c in v))


def group(v):
    return 0 if v[2] == 0 else 1 + side(v[2])


def side(sign):
    return 0 if sign == 1 else 1


def total(terms):
    terms = list(terms)
    while len(terms) > 1:
        terms = [a + b for a, b in zip(terms[::2], terms[1::2])] + terms[len(terms) & ~1 :]
    return terms[0]


def gather(values, span):
    flat = [values[q - span[0]] for q in span if LATTICE[q][2] == 0]
    tilted = [values[q - span[0]] for q in span if LATTICE[q][2]]
    return total(flat) + total(tilted)


def moments(f, g, scale):
    rho, warmth = gather(f, range(19)), gather(g, range(19, 26))
    flow = []
    for axis in range(3):
        result = None
        for q in sorted(range(1, 19, 2), key=lambda q: abs(LATTICE[q][2])):
            if LATTICE[q][axis]:
                odd = f[q] - f[q + 1]
                if result is None:
                    result = odd
                else:
                    result = result + odd if LATTICE[q][axis] == 1 else result - odd
        flow.append(result)
    half = (0.5 * GRAVITY_LIFT * scale) * warmth
    inv = 1.0 / rho
    return rho, warmth, half, (flow[0] * inv, flow[1] * inv, flow[2] * inv + half)


def collide(f, g, scale):
    rho, warmth, half, u = moments(f, g, scale)
    push = rho * half
    rate = 1.0 / TAU_FLOW
    lift = 2.0 * (1.0 - 0.5 / TAU_FLOW)
    weight = WEIGHTS[7] / KEEP_FLOW
    square = u[0] * u[0] + u[1] * u[1] + u[2] * u[2]
    base = (weight * rate * rho) * (1.0 - 1.5 * square) - (3.0 * lift * weight) * (u[2] * push)
    quad = (4.5 * rate * weight) * rho
    line = (3.0 * rate * weight) * rho
    push3 = (3.0 * lift * weight) * push
    push9 = (9.0 * lift * weight) * push
    small = (base, quad, line, push3, push9)
    large = tuple((WEIGHTS[1] / WEIGHTS[7]) * part for part in small)
    post = [None] * 26
    post[0] = f[0] + (WEIGHTS[0] / WEIGHTS[7]) * base
    for q in range(1, 19, 2):
        c = LATTICE[q]
        along = None
        for axis in range(3):
            if c[axis]:
                if along is None:
                    along = u[axis]
                else:
                    along = along + u[axis] if c[axis] == 1 else along - u[axis]
        base, quad, line, push3, push9 = large if q < 7 else small
        inner = quad * along
        odd = line * along
        if c[2] == 1:
            inner, odd = inner + push9, odd + push3
        elif c[2] == -1:
            inner, odd = inner - push9, odd - push3
        even = base + along * inner
        post[q] = f[q] + (even + odd)
        post[q + 1] = f[q + 1] + (even - odd)
    share = 1.0 / (TAU_HEAT * KEEP_HEAT)
    post[19] = g[0] + (WEIGHTS[19] * share) * warmth
    still = (WEIGHTS[20] * share) * warmth
    slope = (4.0 * WEIGHTS[20] * share) * warmth
    for axis in range(3):
        drift = slope * u[axis]
        q = 20 + 2 * axis
        post[q] = g[q - 19] + (still + drift)
        post[q + 1] = g[q - 18] + (still - drift)
    return post


def kernel(
    sizes, flow_in, heat_in, result,
    cur, post, mid, sy, ry, sz, rz, syz, ryz, sums, ledger,
    in_sem, send_sem, recv_sem, sum_send, sum_recv,
):
    count_x, count_y, count_z = sizes
    nx, ny, nz = cur.shape[1:]
    gx, gy, gz = (lax.axis_index(a) for a in ("gx", "gy", "gz"))
    has = {1: gz < count_z - 1, -1: gz > 0}
    everyone = count_x * count_y * count_z
    me = (gx * count_y + gy) * count_z + gz

    def device(v):
        return {
            "gx": lax.rem(gx + v[0] + count_x, count_x),
            "gy": lax.rem(gy + v[1] + count_y, count_y),
            "gz": gz + v[2],
        }

    def ahead(distance):
        other = lax.rem(me + distance, everyone)
        row = other // count_z
        return {"gx": row // count_y, "gy": lax.rem(row, count_y), "gz": lax.rem(other, count_z)}

    def load(part, x):
        return (
            pltpu.make_async_copy(flow_in.at[:, x], cur.at[0:19, x], in_sem.at[part]),
            pltpu.make_async_copy(heat_in.at[:, x], cur.at[19:26, x], in_sem.at[part]),
        )

    loads = [load(0, 0), load(1, nx - 1), [c for x in range(1, nx - 1) for c in load(2, x)]]
    for copies in loads:
        for copy in copies:
            copy.start()

    barrier = pltpu.get_barrier_semaphore()
    near = sorted({(v[0] % count_x, v[1] % count_y, v[2]) for v in LINKS})
    reach = (count_x // 2, count_y // 2, count_z - 1)
    joined = max(reach) <= STEPS and sum(reach) <= 2 * STEPS
    if joined:
        for v in near:
            if v[2] == 0:
                pl.semaphore_signal(barrier, inc=1, device_id=device(v))
        for sign in SIDES:
            @pl.when(has[sign])
            def _():
                for v in near:
                    if v[2] == sign:
                        pl.semaphore_signal(barrier, inc=1, device_id=device(v))
    else:
        @pl.loop(1, everyone)
        def _(d):
            pl.semaphore_signal(barrier, inc=1, device_id=ahead(d))

    def greet():
        if joined:
            count = len([v for v in near if v[2] == 0])
            for sign in SIDES:
                count += jnp.where(has[sign], len([v for v in near if v[2] == sign]), 0)
        else:
            count = everyone - 1
        pl.semaphore_wait(barrier, count)

    lane = lax.broadcasted_iota(jnp.int32, (ny, nz), 1)
    row = lax.broadcasted_iota(jnp.int32, (ny, nz), 0)
    first_row, last_row = row == 0, row == ny - 1
    first_lane, last_lane = lane == 0, lane == nz - 1
    place = lax.rem(lane, FACE)

    def lanes_of(sign, pick):
        mask = None
        for j, q in enumerate(MEMBERS[2, sign]):
            if pick(q):
                mask = place == j if mask is None else mask | (place == j)
        return mask

    def message(s, v):
        x, y, z = v
        if z == 0:
            start = 0 if x == 1 else FACE
            edge, halo = (nx, 0) if x == 1 else (1, nx + 1)
            if y == 0:
                src = post.at[s, start : start + FACE, edge]
                dst = post.at[s, start : start + FACE, halo]
            elif x == 0:
                src = sy.at[s, side(y), :, 1 : nx + 1]
                dst = ry.at[s, side(y), :, 1 : nx + 1]
            else:
                j = MEMBERS[1, y].index(LATTICE.index(v))
                src = sy.at[s, side(y), j, edge]
                dst = ry.at[s, side(y), j, halo]
        elif y == 0:
            src = sz.at[s, side(z), 0 if x == 0 else 1]
            dst = rz.at[s, side(z), 0 if x == 0 else 1 + side(x)]
        else:
            src = syz.at[s, side(z), side(y)]
            dst = ryz.at[s, side(z), side(y)]
        return pltpu.make_async_remote_copy(
            src_ref=src, dst_ref=dst, send_sem=send_sem.at[group(v)], recv_sem=recv_sem.at[s, group(v)],
            device_id=device(v),
        )

    def send(s, links):
        for v in links:
            if v[2] == 0:
                message(s, v).start()
        for sign in SIDES:
            if any(v[2] == sign for v in links):
                @pl.when(has[sign])
                def _():
                    for v in links:
                        if v[2] == sign:
                            message(s, v).start()

    def rows(links):
        count = 0
        for x, y, z in links:
            if y == 0:
                count += FACE * ny if z == 0 else ny
            else:
                count += FACE * nx if x == 0 and z == 0 else 1
        return count

    def settle(sem, count):
        pltpu.make_async_copy(ledger.at[0:count], ledger.at[0:count], sem).wait()

    def receive(s):
        settle(recv_sem.at[s, 0], rows(v for v in LINKS if v[2] == 0))
        for sign in SIDES:
            @pl.when(has[-sign])
            def _():
                settle(recv_sem.at[s, 1 + side(sign)], rows(v for v in LINKS if v[2] == sign))

    def target(x, q):
        return lax.rem(x + (LATTICE[q][0] + nx), nx) * FACE

    def keep_plane(s, x, values, packs):
        for q in range(26):
            post[s, SLOT[q], x + 1] = values[q]
        for sign in SIDES:
            r = ny - 1 if sign == 1 else 0
            for j, q in enumerate(MEMBERS[1, sign]):
                value = values[q]
                if LATTICE[q][2]:
                    value = pltpu.roll(value, LATTICE[q][2] % nz, 1)
                sy[s, side(sign), j, x + 1] = value[r : r + 1, :]
        new = []
        for sign, pack in zip(SIDES, packs):
            source = nz - 1 if sign == 1 else 0
            for j, q in enumerate(MEMBERS[2, sign]):
                k = target(x, q) + j
                turned = pltpu.roll(values[q], lax.rem(k + (nz - source), nz), 1)
                pack = jnp.where(lane == k, turned, pack)
            new.append(pack)
        return tuple(new)

    def stream(s, x):
        for q in range(26):
            cx, cy, cz = LATTICE[q]
            if cy or cz:
                value = post[s, SLOT[q], x + 1]
                if cz:
                    value = pltpu.roll(value, cz % nz, 1)
                if cy:
                    value = pltpu.roll(value, cy % ny, 0)
                mid[SLOT[q], x] = value

    def bounce(s, sign, pack, unit):
        own = MEMBERS[2, sign]
        edge = (nx - 1) * FACE
        wall = pack
        for x in SIDES:
            near_part = pltpu.roll(pack, (-x * FACE) % nz, 1)
            far_part = pltpu.roll(pack, (x * edge) % nz, 1)
            far = lane >= edge if x == 1 else lane < FACE
            wall = jnp.where(
                lanes_of(sign, lambda q: LATTICE[q][0] == x), jnp.where(far, far_part, near_part), wall
            )
        for y in SIDES:
            wall = jnp.where(
                lanes_of(sign, lambda q: LATTICE[q][1] == y), pltpu.roll(pack, -y % ny, 0), wall
            )
        weight = WEIGHTS[own[-1]]
        warm = (2.0 * weight * (COLD_WALL if sign == 1 else HOT_WALL)) * unit
        rz[s, side(-sign), 0] = jnp.where(lanes_of(sign, lambda q: q >= 19), warm - wall, wall)

    def arrive():
        planes = ((0, cur.at[:, 0]), (1, cur.at[:, nx - 1]), (2, cur.at[:, 1 : nx - 1]))
        for part, planes_of in planes:
            pltpu.make_async_copy(planes_of, planes_of, in_sem.at[part]).wait()
            if part:
                yield

    def advance(s, body, arrive, before_send, unit):
        zero = jnp.zeros((ny, nz), jnp.float32)
        packs = (zero, zero)
        stages = iter(arrive() or ())
        next(stages, None)
        for x in (0, nx - 1):
            packs = keep_plane(s, x, body(x, x), packs)
        before_send()
        send(s, [v for v in EARLY if v[2] == 0])
        for sign, pack in zip(SIDES, packs):
            sz[s, side(sign), 1] = pack
        send(s, [v for v in EARLY if v[2]])
        next(stages, None)
        packs = lax.fori_loop(
            1, nx - 1, lambda x, p: keep_plane(s, x, body(x, None), p), packs, unroll=UNROLL
        )
        send(s, [v for v in LATE if v[2] == 0])
        for sign, pack in zip(SIDES, packs):
            whole = pack
            for y in SIDES:
                whole = jnp.where(
                    lanes_of(sign, lambda q: LATTICE[q][1] == y), pltpu.roll(pack, y % ny, 0), whole
                )
            sz[s, side(sign), 0] = whole
            for y in SIDES:
                r = 0 if y == 1 else ny - 1
                syz[s, side(sign), side(y)] = whole[r : r + 1, :]
        send(s, [v for v in LATE if v[2]])
        for sign in SIDES:
            @pl.when(jnp.logical_not(has[sign]))
            def _():
                bounce(s, sign, sz[s, side(sign), 0], unit)
        lax.fori_loop(0, nx, lambda x, c: (stream(s, x), c)[1], 0, unroll=2)

    def columns(s):
        result = {}
        for sign in SIDES:
            tile = rz[s, side(sign), 0]
            for x in SIDES:
                j = [q for q in MEMBERS[2, sign] if LATTICE[q][0] == x]
                k = (0 if x == 1 else nx - 1) * FACE + MEMBERS[2, sign].index(j[0])
                tile = jnp.where((lane == k) & has[-sign], rz[s, side(sign), 1 + side(x)], tile)
            for y in SIDES:
                mask = lanes_of(sign, lambda q: LATTICE[q][1] == y) & (first_row if y == 1 else last_row)
                edge = jnp.broadcast_to(ryz[s, side(sign), side(y)], (ny, nz))
                tile = jnp.where(mask & has[-sign], edge, tile)
            result[sign] = tile
        return result

    def pull(s, x, fixed, beyond, q):
        cx, cy, cz = LATTICE[q]
        at = x - cx + 1
        if fixed is not None and fixed - cx in (-1, nx):
            value = post[s, SLOT[q], at]
            if cz:
                value = pltpu.roll(value, cz % nz, 1)
            if cy:
                value = pltpu.roll(value, cy % ny, 0)
        elif cy or cz:
            value = mid[SLOT[q], at - 1]
        else:
            value = post[s, SLOT[q], at]
        if cy:
            j = MEMBERS[1, cy].index(q)
            edge = jnp.broadcast_to(ry[s, side(cy), j, at], (ny, nz))
            value = jnp.where(first_row if cy == 1 else last_row, edge, value)
        if cz:
            j = MEMBERS[2, cz].index(q)
            end = 0 if cz == 1 else nz - 1
            outer = pltpu.roll(beyond[cz], lax.rem(end + nz - (x * FACE + j), nz), 1)
            value = jnp.where(first_lane if cz == 1 else last_lane, outer, value)
        return value

    def fresh(x, fixed):
        return collide([cur[q, x] for q in range(19)], [cur[q, x] for q in range(19, 26)], 1.0)

    advance(0, fresh, arrive, greet, 1.0 / KEEP_HEAT)

    def step(s, carry):
        scale, unit = carry
        receive(s)
        beyond = columns(s)

        def body(x, fixed):
            values = [pull(s, x, fixed, beyond, q) for q in range(26)]
            return collide(values[:19], values[19:], scale)

        unit = unit * (1.0 / KEEP_HEAT)
        advance(s + 1, body, lambda: None, lambda: None, unit)
        return scale * KEEP_HEAT, unit

    lax.fori_loop(0, STEPS - 1, step, (jnp.float32(KEEP_HEAT), jnp.float32(1.0 / KEEP_HEAT)))

    last = STEPS - 1
    receive(last)
    beyond = columns(last)

    def finish(x, fixed, flux):
        values = [pull(last, x, fixed, beyond, q) for q in range(26)]
        for q in range(26):
            result[q, x] = (KEEP_FLOW if q < 19 else KEEP_HEAT) ** STEPS * values[q]
        _, warmth, _, u = moments(values[:19], values[19:], KEEP_HEAT**STEPS)
        return flux + u[2] * warmth

    flux = jnp.zeros((ny, nz), jnp.float32)
    for x in (0, nx - 1):
        flux = finish(x, x, flux)
    flux = lax.fori_loop(1, nx - 1, lambda x, t: finish(x, None, t), flux, unroll=UNROLL)
    sums[me] = jnp.sum(flux, axis=0, keepdims=True)

    def send_sum(target):
        pltpu.make_async_remote_copy(
            src_ref=sums.at[me], dst_ref=sums.at[me],
            send_sem=sum_send, recv_sem=sum_recv, device_id=target,
        ).start()

    if joined:
        xs, ys, zs = (
            [lax.rem(at + d, n) for d in range(n)] for at, n in zip((gx, gy, gz), sizes)
        )
        for dz in reversed(range(count_z)):
            for dx in reversed(range(count_x)):
                for dy in reversed(range(count_y)):
                    if dx or dy or dz:
                        send_sum({"gx": xs[dx], "gy": ys[dy], "gz": zs[dz]})
    else:
        pl.loop(1, everyone)(lambda d: send_sum(ahead(d)))

    settle(send_sem.at[0], STEPS * rows(v for v in LINKS if v[2] == 0))
    for sign in SIDES:
        @pl.when(has[sign])
        def _():
            settle(send_sem.at[1 + side(sign)], STEPS * rows(v for v in LINKS if v[2] == sign))
    all_rows = pltpu.make_async_remote_copy(
        src_ref=sums.at[pl.ds(0, everyone - 1)], dst_ref=sums.at[pl.ds(0, everyone - 1)],
        send_sem=sum_send, recv_sem=sum_recv, device_id=ahead(1),
    )
    all_rows.wait_send()
    all_rows.wait_recv()
    result[26, 0, 0:1, :] = jnp.sum(sums[...], axis=0)


def write_out(scale, result, flow_out, heat_out, nusselt_out, small, sem):
    copies = (
        pltpu.make_async_copy(result.at[0:19], flow_out, sem.at[0]),
        pltpu.make_async_copy(result.at[19:26], heat_out, sem.at[1]),
        pltpu.make_async_copy(small, nusselt_out, sem.at[2]),
    )
    for copy in copies[:2]:
        copy.start()
    small[...] = 1.0 + scale * jnp.sum(result[26, 0, 0:1, :], axis=1, keepdims=True)
    copies[2].start()
    for copy in copies:
        copy.wait()


def per_device(sizes, flow_pops, heat_pops):
    nx, ny, nz = flow_pops.shape[1:]
    count_x, count_y, count_z = sizes
    f32 = jnp.float32
    dma = pltpu.SemaphoreType.DMA
    cells = nx * ny * nz * count_x * count_y * count_z
    scale = nz * count_z / (DIFFUSIVITY * (HOT_WALL - COLD_WALL)) / cells * KEEP_HEAT**STEPS
    hbm = pl.BlockSpec(memory_space=pltpu.HBM)
    vmem = pl.BlockSpec(memory_space=pltpu.VMEM)
    result = pl.pallas_call(
        functools.partial(kernel, sizes),
        out_shape=pltpu.VMEM((27, nx, ny, nz), f32),
        in_specs=[hbm, hbm],
        out_specs=vmem,
        scratch_shapes=[
            pltpu.VMEM((26, nx, ny, nz), f32),
            pltpu.VMEM((STEPS, 26, nx + 2, ny, nz), f32),
            pltpu.VMEM((26, nx, ny, nz), f32),
            pltpu.VMEM((STEPS, 2, FACE, nx + 2, 1, nz), f32),
            pltpu.VMEM((STEPS, 2, FACE, nx + 2, 1, nz), f32),
            pltpu.VMEM((STEPS, 2, 2, ny, nz), f32),
            pltpu.VMEM((STEPS, 2, 3, ny, nz), f32),
            pltpu.VMEM((STEPS, 2, 2, 1, nz), f32),
            pltpu.VMEM((STEPS, 2, 2, 1, nz), f32),
            pltpu.VMEM((count_x * count_y * count_z, 1, nz), f32),
            pltpu.VMEM((STEPS * 2 * (FACE * (nx + ny) + 2), 1, nz), f32),
            dma((3,)),
            dma((3,)),
            dma((STEPS, 3)),
            dma,
            dma,
        ],
        compiler_params=pltpu.CompilerParams(
            collective_id=0, has_side_effects=True, vmem_limit_bytes=55000000
        ),
    )(pltpu.with_memory_space_constraint(flow_pops, pltpu.HBM), pltpu.with_memory_space_constraint(heat_pops, pltpu.HBM))
    flow, heat, nusselt = pl.pallas_call(
        functools.partial(write_out, scale),
        out_shape=(
            jax.ShapeDtypeStruct(flow_pops.shape, f32),
            jax.ShapeDtypeStruct(heat_pops.shape, f32),
            jax.ShapeDtypeStruct((1, 1), f32),
        ),
        in_specs=[vmem],
        out_specs=(hbm, hbm, hbm),
        scratch_shapes=[pltpu.VMEM((1, 1), f32), dma((3,))],
        compiler_params=pltpu.CompilerParams(vmem_limit_bytes=1024 * 1024),
    )(result)
    return flow, heat, nusselt.reshape(())


def solution(mesh):
    placed = P(None, "gx", "gy", "gz")
    sizes = tuple(mesh.shape[a] for a in ("gx", "gy", "gz"))
    return jax.shard_map(
        functools.partial(per_device, sizes),
        mesh=mesh,
        in_specs=(placed, placed),
        out_specs=(placed, placed, P()),
        check_vma=False,
    )
```

time: 24.9 us -> 23.5 us (0.944)
  Pallas kernels: 24.2 us -> 22.7 us
    pallas_call x1, Pallas kernels: 23 us -> 21.8 us  [per_device(): pl.pallas_call(functools.partial(kernel, sizes), out_shape=pltpu.VMEM((27...]
where the time goes in v2:
time: 23.5 us; the launch traced here: 23.3 us
  Pallas kernels  22.7 us (97%)
  between operations  0.64 us (3%)
    pallas_call x1, Pallas kernels, per_device(): pl.pallas_call(functools.partial(kernel, sizes), out_shape=pltpu.VMEM((27...  21.8 us
    pallas_call x1, Pallas kernels, per_device(): pl.pallas_call(functools.partial(write_out, scale), out_shape=(jax.ShapeD...  0.92 us

profile of v2, /device:TPU:0, one launch (start us, length us, event | category | flops | bytes accessed | tf_op | source)
XLA Modules:
  0.0 23.3 jit_solution(1613219937317163707)
XLA Ops:
  0.6 21.8 %shard_map.49.result = f32[27,8,8,128]{3,2,1,0:T(8,128)S(1)} custom-call(f32[19,8,8,128]{3,2,1,0:T(8,128)} %flow_in.1, f32[7,8,8,128]{3,2,1,0:T(8,128)} %heat_in.1), custom_call_target="tpu_custom_call" | custom-call | tf_op jit(solution)/shard_map/pallas_call | solution.py:518
  22.4 0.9 %shard_map.50 = (f32[19,8,8,128]{3,2,1,0:T(8,128)}, f32[7,8,8,128]{3,2,1,0:T(8,128)}, f32[1,1]{1,0:T(1,128)}) custom-call(f32[27,8,8,128]{3,2,1,0:T(8,128)S(1)} %shard_map.49.result), custom_call_target="tpu_custom_call" | custom-call | tf_op jit(solution)/shard_map/pallas_call | solution.py:545

commit v3 on v2

--- a/solution.py
+++ b/solution.py
@@ -159,7 +159,7 @@
 
 def kernel(
     sizes, flow_in, heat_in, result,
-    cur, post, mid, sy, ry, sz, rz, syz, ryz, sums, ledger,
+    cur, post, mid, sy, ry, sz, rz, sxz, rxz, syz, ryz, sums, ledger,
     in_sem, send_sem, recv_sem, sum_send, sum_recv,
 ):
     count_x, count_y, count_z = sizes
@@ -225,6 +225,7 @@
     first_row, last_row = row == 0, row == ny - 1
     first_lane, last_lane = lane == 0, lane == nz - 1
     place = lax.rem(lane, FACE)
+    slant = {1: lane == lax.rem(nz - row, nz), -1: lane == nz - 1 - row}
 
     def lanes_of(sign, pick):
         mask = None
@@ -249,8 +250,8 @@
                 src = sy.at[s, side(y), j, edge]
                 dst = ry.at[s, side(y), j, halo]
         elif y == 0:
-            src = sz.at[s, side(z), 0 if x == 0 else 1]
-            dst = rz.at[s, side(z), 0 if x == 0 else 1 + side(x)]
+            src = sz.at[s, side(z)] if x == 0 else sxz.at[s, side(z), side(x)]
+            dst = rz.at[s, side(z)] if x == 0 else rxz.at[s, side(z), side(x)]
         else:
             src = syz.at[s, side(z), side(y)]
             dst = ryz.at[s, side(z), side(y)]
@@ -275,7 +276,7 @@
         count = 0
         for x, y, z in links:
             if y == 0:
-                count += FACE * ny if z == 0 else ny
+                count += FACE * ny if z == 0 else ny if x == 0 else 1
             else:
                 count += FACE * nx if x == 0 and z == 0 else 1
         return count
@@ -289,6 +290,10 @@
             @pl.when(has[-sign])
             def _():
                 settle(recv_sem.at[s, 1 + side(sign)], rows(v for v in LINKS if v[2] == sign))
+
+    def flatten(sign, tile, at):
+        column = jnp.broadcast_to(tile[:, at : at + 1], (ny, nz))
+        return jnp.sum(jnp.where(slant[sign], column, 0.0), axis=0, keepdims=True)
 
     def target(x, q):
         return lax.rem(x + (LATTICE[q][0] + nx), nx) * FACE
@@ -341,7 +346,12 @@
             )
         weight = WEIGHTS[own[-1]]
         warm = (2.0 * weight * (COLD_WALL if sign == 1 else HOT_WALL)) * unit
-        rz[s, side(-sign), 0] = jnp.where(lanes_of(sign, lambda q: q >= 19), warm - wall, wall)
+        wall = jnp.where(lanes_of(sign, lambda q: q >= 19), warm - wall, wall)
+        rz[s, side(-sign)] = wall
+        for x in SIDES:
+            q = LATTICE.index((x, 0, -sign))
+            at = (0 if x == 1 else nx - 1) * FACE + MEMBERS[2, -sign].index(q)
+            rxz[s, side(-sign), side(x)] = flatten(-sign, wall, at)
 
     def arrive():
         planes = ((0, cur.at[:, 0]), (1, cur.at[:, nx - 1]), (2, cur.at[:, 1 : nx - 1]))
@@ -356,11 +366,14 @@
         stages = iter(arrive() or ())
         next(stages, None)
         for x in (0, nx - 1):
-            packs = keep_plane(s, x, body(x, x), packs)
+            values = body(x, x)
+            packs = keep_plane(s, x, values, packs)
+            for sign in SIDES:
+                v = (1 if x else -1, 0, sign)
+                sxz[s, side(sign), side(v[0])] = flatten(sign, values[LATTICE.index(v)], nz - 1 if sign == 1 else 0)
         before_send()
-        send(s, [v for v in EARLY if v[2] == 0])
-        for sign, pack in zip(SIDES, packs):
-            sz[s, side(sign), 1] = pack
+        send(s, [v for v in EARLY if v[1] and not v[2]])
+        send(s, [v for v in EARLY if not v[1] and not v[2]])
         send(s, [v for v in EARLY if v[2]])
         next(stages, None)
         packs = lax.fori_loop(
@@ -373,7 +386,7 @@
                 whole = jnp.where(
                     lanes_of(sign, lambda q: LATTICE[q][1] == y), pltpu.roll(pack, y % ny, 0), whole
                 )
-            sz[s, side(sign), 0] = whole
+            sz[s, side(sign)] = whole
             for y in SIDES:
                 r = 0 if y == 1 else ny - 1
                 syz[s, side(sign), side(y)] = whole[r : r + 1, :]
@@ -381,17 +394,13 @@
         for sign in SIDES:
             @pl.when(jnp.logical_not(has[sign]))
             def _():
-                bounce(s, sign, sz[s, side(sign), 0], unit)
+                bounce(s, sign, sz[s, side(sign)], unit)
         lax.fori_loop(0, nx, lambda x, c: (stream(s, x), c)[1], 0, unroll=2)
 
     def columns(s):
         result = {}
         for sign in SIDES:
-            tile = rz[s, side(sign), 0]
-            for x in SIDES:
-                j = [q for q in MEMBERS[2, sign] if LATTICE[q][0] == x]
-                k = (0 if x == 1 else nx - 1) * FACE + MEMBERS[2, sign].index(j[0])
-                tile = jnp.where((lane == k) & has[-sign], rz[s, side(sign), 1 + side(x)], tile)
+            tile = rz[s, side(sign)]
             for y in SIDES:
                 mask = lanes_of(sign, lambda q: LATTICE[q][1] == y) & (first_row if y == 1 else last_row)
                 edge = jnp.broadcast_to(ryz[s, side(sign), side(y)], (ny, nz))
@@ -419,7 +428,11 @@
         if cz:
             j = MEMBERS[2, cz].index(q)
             end = 0 if cz == 1 else nz - 1
-            outer = pltpu.roll(beyond[cz], lax.rem(end + nz - (x * FACE + j), nz), 1)
+            if fixed is not None and fixed - cx in (-1, nx):
+                line = jnp.broadcast_to(rxz[s, side(cz), side(cx)], (ny, nz))
+                outer = pltpu.roll(line, 0, 1, stride=1, stride_axis=0)
+            else:
+                outer = pltpu.roll(beyond[cz], lax.rem(end + nz - (x * FACE + j), nz), 1)
             value = jnp.where(first_lane if cz == 1 else last_lane, outer, value)
         return value
 
@@ -526,8 +539,10 @@
             pltpu.VMEM((26, nx, ny, nz), f32),
             pltpu.VMEM((STEPS, 2, FACE, nx + 2, 1, nz), f32),
             pltpu.VMEM((STEPS, 2, FACE, nx + 2, 1, nz), f32),
-            pltpu.VMEM((STEPS, 2, 2, ny, nz), f32),
-            pltpu.VMEM((STEPS, 2, 3, ny, nz), f32),
+            pltpu.VMEM((STEPS, 2, ny, nz), f32),
+            pltpu.VMEM((STEPS, 2, ny, nz), f32),
+            pltpu.VMEM((STEPS, 2, 2, 1, nz), f32),
+            pltpu.VMEM((STEPS, 2, 2, 1, nz), f32),
             pltpu.VMEM((STEPS, 2, 2, 1, nz), f32),
             pltpu.VMEM((STEPS, 2, 2, 1, nz), f32),
             pltpu.VMEM((count_x * count_y * count_z, 1, nz), f32),

time: 23.5 us -> 22.2 us (0.945)
  Pallas kernels: 22.7 us -> 21.4 us
    pallas_call x1, Pallas kernels: 21.8 us -> 20.5 us  [per_device(): pl.pallas_call(functools.partial(kernel, sizes), out_shape=pltpu.VMEM((27...]
where the time goes in v3:
time: 22.2 us; the launch traced here: 22 us
  Pallas kernels  21.4 us (96%)
  between operations  0.64 us (3%)
    pallas_call x1, Pallas kernels, per_device(): pl.pallas_call(functools.partial(kernel, sizes), out_shape=pltpu.VMEM((27...  20.5 us
    pallas_call x1, Pallas kernels, per_device(): pl.pallas_call(functools.partial(write_out, scale), out_shape=(jax.ShapeD...  0.92 us

profile of v3, /device:TPU:0, one launch (start us, length us, event | category | flops | bytes accessed | tf_op | source)
XLA Modules:
  0.0 22.0 jit_solution(563061374264810399)
XLA Ops:
  0.6 20.5 %shard_map.49.result = f32[27,8,8,128]{3,2,1,0:T(8,128)S(1)} custom-call(f32[19,8,8,128]{3,2,1,0:T(8,128)} %flow_in.1, f32[7,8,8,128]{3,2,1,0:T(8,128)} %heat_in.1), custom_call_target="tpu_custom_call" | custom-call | tf_op jit(solution)/shard_map/pallas_call | solution.py:531
  21.1 0.9 %shard_map.50 = (f32[19,8,8,128]{3,2,1,0:T(8,128)}, f32[7,8,8,128]{3,2,1,0:T(8,128)}, f32[1,1]{1,0:T(1,128)}) custom-call(f32[27,8,8,128]{3,2,1,0:T(8,128)S(1)} %shard_map.49.result), custom_call_target="tpu_custom_call" | custom-call | tf_op jit(solution)/shard_map/pallas_call | solution.py:560

commit v4 on v3

--- a/solution.py
+++ b/solution.py
@@ -187,29 +187,41 @@
             pltpu.make_async_copy(heat_in.at[:, x], cur.at[19:26, x], in_sem.at[part]),
         )
 
-    loads = [load(0, 0), load(1, nx - 1), [c for x in range(1, nx - 1) for c in load(2, x)]]
-    for copies in loads:
-        for copy in copies:
-            copy.start()
-
+    def pieces(part, x):
+        cuts = (0, 7, 13, 19)
+        return [
+            pltpu.make_async_copy(flow_in.at[a:b, x], cur.at[a:b, x], in_sem.at[part])
+            for a, b in zip(cuts, cuts[1:])
+        ] + [pltpu.make_async_copy(heat_in.at[:, x], cur.at[19:26, x], in_sem.at[part])]
+
+    loads = [pieces(0, 0), pieces(1, nx - 1), [c for x in range(1, nx - 1) for c in load(2, x)]]
+    def fetch(parts):
+        for copies in parts:
+            for copy in copies:
+                copy.start()
+
+    fetch(loads[:2])
     barrier = pltpu.get_barrier_semaphore()
-    near = sorted({(v[0] % count_x, v[1] % count_y, v[2]) for v in LINKS})
+    near = sorted(
+        {(v[0] % count_x, v[1] % count_y, v[2]) for v in LINKS}, key=lambda v: -sum(c != 0 for c in v)
+    )
     reach = (count_x // 2, count_y // 2, count_z - 1)
     joined = max(reach) <= STEPS and sum(reach) <= 2 * STEPS
     if joined:
-        for v in near:
-            if v[2] == 0:
-                pl.semaphore_signal(barrier, inc=1, device_id=device(v))
         for sign in SIDES:
             @pl.when(has[sign])
             def _():
                 for v in near:
                     if v[2] == sign:
                         pl.semaphore_signal(barrier, inc=1, device_id=device(v))
+        for v in near:
+            if v[2] == 0:
+                pl.semaphore_signal(barrier, inc=1, device_id=device(v))
     else:
         @pl.loop(1, everyone)
         def _(d):
             pl.semaphore_signal(barrier, inc=1, device_id=ahead(d))
+    fetch(loads[2:])
 
     def greet():
         if joined:
@@ -298,12 +310,23 @@
     def target(x, q):
         return lax.rem(x + (LATTICE[q][0] + nx), nx) * FACE
 
-    def keep_plane(s, x, values, packs):
+    def keep_urgent(s, x, way, values):
+        for q in MEMBERS[0, way]:
+            post[s, SLOT[q], x + 1] = values[q]
+        for y in SIDES:
+            q = LATTICE.index((way, y, 0))
+            r = ny - 1 if y == 1 else 0
+            sy[s, side(y), MEMBERS[1, y].index(q), x + 1] = values[q][r : r + 1, :]
+
+    def keep_plane(s, x, way, values, packs):
         for q in range(26):
-            post[s, SLOT[q], x + 1] = values[q]
+            if LATTICE[q][0] != way:
+                post[s, SLOT[q], x + 1] = values[q]
         for sign in SIDES:
             r = ny - 1 if sign == 1 else 0
             for j, q in enumerate(MEMBERS[1, sign]):
+                if LATTICE[q][0] == way:
+                    continue
                 value = values[q]
                 if LATTICE[q][2]:
                     value = pltpu.roll(value, LATTICE[q][2] % nz, 1)
@@ -365,19 +388,24 @@
         packs = (zero, zero)
         stages = iter(arrive() or ())
         next(stages, None)
-        for x in (0, nx - 1):
+        first = []
+        for x, way in ((0, -1), (nx - 1, 1)):
             values = body(x, x)
-            packs = keep_plane(s, x, values, packs)
+            first.append((x, way, values))
+            keep_urgent(s, x, way, values)
+        before_send()
+        send(s, [v for v in EARLY if v[1]])
+        send(s, [v for v in EARLY if not v[1] and not v[2]])
+        for x, way, values in first:
             for sign in SIDES:
-                v = (1 if x else -1, 0, sign)
-                sxz[s, side(sign), side(v[0])] = flatten(sign, values[LATTICE.index(v)], nz - 1 if sign == 1 else 0)
-        before_send()
-        send(s, [v for v in EARLY if v[1] and not v[2]])
-        send(s, [v for v in EARLY if not v[1] and not v[2]])
+                value = values[LATTICE.index((way, 0, sign))]
+                sxz[s, side(sign), side(way)] = flatten(sign, value, nz - 1 if sign == 1 else 0)
         send(s, [v for v in EARLY if v[2]])
+        for x, way, values in first:
+            packs = keep_plane(s, x, way, values, packs)
         next(stages, None)
         packs = lax.fori_loop(
-            1, nx - 1, lambda x, p: keep_plane(s, x, body(x, None), p), packs, unroll=UNROLL
+            1, nx - 1, lambda x, p: keep_plane(s, x, None, body(x, None), p), packs, unroll=UNROLL
         )
         send(s, [v for v in LATE if v[2] == 0])
         for sign, pack in zip(SIDES, packs):
@@ -480,14 +508,16 @@
         ).start()
 
     if joined:
-        xs, ys, zs = (
-            [lax.rem(at + d, n) for d in range(n)] for at, n in zip((gx, gy, gz), sizes)
-        )
-        for dz in reversed(range(count_z)):
+        xs, ys = ([lax.rem(at + d, n) for d in range(n)] for at, n in zip((gx, gy), sizes))
+        for k in range(count_z):
+            z = jnp.where(2 * gz >= count_z, k, count_z - 1 - k)
             for dx in reversed(range(count_x)):
                 for dy in reversed(range(count_y)):
-                    if dx or dy or dz:
-                        send_sum({"gx": xs[dx], "gy": ys[dy], "gz": zs[dz]})
+                    there = {"gx": xs[dx], "gy": ys[dy], "gz": z}
+                    if dx or dy:
+                        send_sum(there)
+                    else:
+                        pl.when(z != gz)(functools.partial(send_sum, there))
     else:
         pl.loop(1, everyone)(lambda d: send_sum(ahead(d)))
 
@@ -506,17 +536,16 @@
 
 
 def write_out(scale, result, flow_out, heat_out, nusselt_out, small, sem):
-    copies = (
-        pltpu.make_async_copy(result.at[0:19], flow_out, sem.at[0]),
-        pltpu.make_async_copy(result.at[19:26], heat_out, sem.at[1]),
-        pltpu.make_async_copy(small, nusselt_out, sem.at[2]),
-    )
-    for copy in copies[:2]:
-        copy.start()
+    flow_cuts, heat_cuts = (0, 4, 8, 12, 16, 19), (0, 4, 7)
+    for a, b in zip(flow_cuts, flow_cuts[1:]):
+        pltpu.make_async_copy(result.at[a:b], flow_out.at[a:b], sem.at[0]).start()
+    for a, b in zip(heat_cuts, heat_cuts[1:]):
+        pltpu.make_async_copy(result.at[19 + a : 19 + b], heat_out.at[a:b], sem.at[0]).start()
     small[...] = 1.0 + scale * jnp.sum(result[26, 0, 0:1, :], axis=1, keepdims=True)
-    copies[2].start()
-    for copy in copies:
-        copy.wait()
+    number = pltpu.make_async_copy(small, nusselt_out, sem.at[1])
+    number.start()
+    pltpu.make_async_copy(result.at[0:26], result.at[0:26], sem.at[0]).wait()
+    number.wait()
 
 
 def per_device(sizes, flow_pops, heat_pops):
@@ -566,7 +595,7 @@
         ),
         in_specs=[vmem],
         out_specs=(hbm, hbm, hbm),
-        scratch_shapes=[pltpu.VMEM((1, 1), f32), dma((3,))],
+        scratch_shapes=[pltpu.VMEM((1, 1), f32), dma((2,))],
         compiler_params=pltpu.CompilerParams(vmem_limit_bytes=1024 * 1024),
     )(result)
     return flow, heat, nusselt.reshape(())

time: 22.2 us -> 21.9 us (0.986)
  Pallas kernels: 21.4 us -> 21.1 us
    pallas_call x1, Pallas kernels: 20.5 us -> 20.2 us  [per_device(): pl.pallas_call(functools.partial(kernel, sizes), out_shape=pltpu.VMEM((27...]
where the time goes in v4:
time: 21.9 us; the launch traced here: 21.8 us
  Pallas kernels  21.1 us (96%)
  between operations  0.64 us (3%)
    pallas_call x1, Pallas kernels, per_device(): pl.pallas_call(functools.partial(kernel, sizes), out_shape=pltpu.VMEM((27...  20.2 us
    pallas_call x1, Pallas kernels, per_device(): pl.pallas_call(functools.partial(write_out, scale), out_shape=(jax.ShapeD...  0.91 us

profile of v4, /device:TPU:0, one launch (start us, length us, event | category | flops | bytes accessed | tf_op | source)
XLA Modules:
  0.0 21.8 jit_solution(4935472814213789345)
XLA Ops:
  0.6 20.2 %shard_map.49.result = f32[27,8,8,128]{3,2,1,0:T(8,128)S(1)} custom-call(f32[19,8,8,128]{3,2,1,0:T(8,128)} %flow_in.1, f32[7,8,8,128]{3,2,1,0:T(8,128)} %heat_in.1), custom_call_target="tpu_custom_call" | custom-call | tf_op jit(solution)/shard_map/pallas_call | solution.py:560
  20.8 0.9 %shard_map.50 = (f32[19,8,8,128]{3,2,1,0:T(8,128)}, f32[7,8,8,128]{3,2,1,0:T(8,128)}, f32[1,1]{1,0:T(1,128)}) custom-call(f32[27,8,8,128]{3,2,1,0:T(8,128)S(1)} %shard_map.49.result), custom_call_target="tpu_custom_call" | custom-call | tf_op jit(solution)/shard_map/pallas_call | solution.py:589

commit v5 on v4

--- a/solution.py
+++ b/solution.py
@@ -159,7 +159,7 @@
 
 def kernel(
     sizes, flow_in, heat_in, result,
-    cur, post, mid, sy, ry, sz, rz, sxz, rxz, syz, ryz, sums, ledger,
+    cur, post, mid, sx, rx, sy, ry, sz, rz, sxz, rxz, syz, ryz, sums, ledger,
     in_sem, send_sem, recv_sem, sum_send, sum_recv,
 ):
     count_x, count_y, count_z = sizes
@@ -246,14 +246,15 @@
                 mask = place == j if mask is None else mask | (place == j)
         return mask
 
+    paired = count_x == 2
+
     def message(s, v):
         x, y, z = v
         if z == 0:
             start = 0 if x == 1 else FACE
             edge, halo = (nx, 0) if x == 1 else (1, nx + 1)
             if y == 0:
-                src = post.at[s, start : start + FACE, edge]
-                dst = post.at[s, start : start + FACE, halo]
+                src, dst = (sx.at[s], rx.at[s]) if paired else (sx.at[s, side(x)], rx.at[s, side(x)])
             elif x == 0:
                 src = sy.at[s, side(y), :, 1 : nx + 1]
                 dst = ry.at[s, side(y), :, 1 : nx + 1]
@@ -262,8 +263,12 @@
                 src = sy.at[s, side(y), j, edge]
                 dst = ry.at[s, side(y), j, halo]
         elif y == 0:
-            src = sz.at[s, side(z)] if x == 0 else sxz.at[s, side(z), side(x)]
-            dst = rz.at[s, side(z)] if x == 0 else rxz.at[s, side(z), side(x)]
+            if x == 0:
+                src, dst = sz.at[s, side(z)], rz.at[s, side(z)]
+            elif paired:
+                src, dst = sxz.at[s, side(z)], rxz.at[s, side(z)]
+            else:
+                src, dst = sxz.at[s, side(z), side(x)], rxz.at[s, side(z), side(x)]
         else:
             src = syz.at[s, side(z), side(y)]
             dst = ryz.at[s, side(z), side(y)]
@@ -273,6 +278,7 @@
         )
 
     def send(s, links):
+        links = [v for v in links if not (paired and v[0] == -1 and v[1] == 0)]
         for v in links:
             if v[2] == 0:
                 message(s, v).start()
@@ -311,8 +317,8 @@
         return lax.rem(x + (LATTICE[q][0] + nx), nx) * FACE
 
     def keep_urgent(s, x, way, values):
-        for q in MEMBERS[0, way]:
-            post[s, SLOT[q], x + 1] = values[q]
+        for j, q in enumerate(MEMBERS[0, way]):
+            sx[s, side(way), j] = values[q]
         for y in SIDES:
             q = LATTICE.index((way, y, 0))
             r = ny - 1 if y == 1 else 0
@@ -440,7 +446,7 @@
         cx, cy, cz = LATTICE[q]
         at = x - cx + 1
         if fixed is not None and fixed - cx in (-1, nx):
-            value = post[s, SLOT[q], at]
+            value = rx[s, side(cx), MEMBERS[0, cx].index(q)]
             if cz:
                 value = pltpu.roll(value, cz % nz, 1)
             if cy:
@@ -566,6 +572,8 @@
             pltpu.VMEM((26, nx, ny, nz), f32),
             pltpu.VMEM((STEPS, 26, nx + 2, ny, nz), f32),
             pltpu.VMEM((26, nx, ny, nz), f32),
+            pltpu.VMEM((STEPS, 2, FACE, ny, nz), f32),
+            pltpu.VMEM((STEPS, 2, FACE, ny, nz), f32),
             pltpu.VMEM((STEPS, 2, FACE, nx + 2, 1, nz), f32),
             pltpu.VMEM((STEPS, 2, FACE, nx + 2, 1, nz), f32),
             pltpu.VMEM((STEPS, 2, ny, nz), f32),

time: 21.9 us -> 21.7 us (level)
  no operation moved by 1% of the time
where the time goes in v5:
time: 21.7 us; the launch traced here: 21.6 us
  Pallas kernels  20.9 us (96%)
  between operations  0.64 us (3%)
    pallas_call x1, Pallas kernels, per_device(): pl.pallas_call(functools.partial(kernel, sizes), out_shape=pltpu.VMEM((27...  20 us
    pallas_call x1, Pallas kernels, per_device(): pl.pallas_call(functools.partial(write_out, scale), out_shape=(jax.ShapeD...  0.91 us

profile of v5, /device:TPU:0, one launch (start us, length us, event | category | flops | bytes accessed | tf_op | source)
XLA Modules:
  0.0 21.6 jit_solution(8141044192338754895)
XLA Ops:
  0.6 20.0 %shard_map.49.result = f32[27,8,8,128]{3,2,1,0:T(8,128)S(1)} custom-call(f32[19,8,8,128]{3,2,1,0:T(8,128)} %flow_in.1, f32[7,8,8,128]{3,2,1,0:T(8,128)} %heat_in.1), custom_call_target="tpu_custom_call" | custom-call | tf_op jit(solution)/shard_map/pallas_call | solution.py:566
  20.7 0.9 %shard_map.50 = (f32[19,8,8,128]{3,2,1,0:T(8,128)}, f32[7,8,8,128]{3,2,1,0:T(8,128)}, f32[1,1]{1,0:T(1,128)}) custom-call(f32[27,8,8,128]{3,2,1,0:T(8,128)S(1)} %shard_map.49.result), custom_call_target="tpu_custom_call" | custom-call | tf_op jit(solution)/shard_map/pallas_call | solution.py:597

commit v6 on v5

--- a/solution.py
+++ b/solution.py
@@ -159,7 +159,7 @@
 
 def kernel(
     sizes, flow_in, heat_in, result,
-    cur, post, mid, sx, rx, sy, ry, sz, rz, sxz, rxz, syz, ryz, sums, ledger,
+    cur, post, mid, sx, rx, sy, ry, sz, rz, sxy, rxy, sxz, rxz, syz, ryz, sums, ledger,
     in_sem, send_sem, recv_sem, sum_send, sum_recv,
 ):
     count_x, count_y, count_z = sizes
@@ -251,17 +251,15 @@
     def message(s, v):
         x, y, z = v
         if z == 0:
-            start = 0 if x == 1 else FACE
-            edge, halo = (nx, 0) if x == 1 else (1, nx + 1)
             if y == 0:
                 src, dst = (sx.at[s], rx.at[s]) if paired else (sx.at[s, side(x)], rx.at[s, side(x)])
             elif x == 0:
                 src = sy.at[s, side(y), :, 1 : nx + 1]
                 dst = ry.at[s, side(y), :, 1 : nx + 1]
             else:
-                j = MEMBERS[1, y].index(LATTICE.index(v))
-                src = sy.at[s, side(y), j, edge]
-                dst = ry.at[s, side(y), j, halo]
+                src, dst = sxy.at[s, side(y)], rxy.at[s, side(y)]
+                if not paired:
+                    src, dst = src.at[side(x)], dst.at[side(x)]
         elif y == 0:
             if x == 0:
                 src, dst = sz.at[s, side(z)], rz.at[s, side(z)]
@@ -278,7 +276,7 @@
         )
 
     def send(s, links):
-        links = [v for v in links if not (paired and v[0] == -1 and v[1] == 0)]
+        links = [v for v in links if not (paired and v[0] == -1)]
         for v in links:
             if v[2] == 0:
                 message(s, v).start()
@@ -322,7 +320,7 @@
         for y in SIDES:
             q = LATTICE.index((way, y, 0))
             r = ny - 1 if y == 1 else 0
-            sy[s, side(y), MEMBERS[1, y].index(q), x + 1] = values[q][r : r + 1, :]
+            sxy[s, side(y), side(way)] = values[q][r : r + 1, :]
 
     def keep_plane(s, x, way, values, packs):
         for q in range(26):
@@ -457,7 +455,11 @@
             value = post[s, SLOT[q], at]
         if cy:
             j = MEMBERS[1, cy].index(q)
-            edge = jnp.broadcast_to(ry[s, side(cy), j, at], (ny, nz))
+            if fixed is not None and fixed - cx in (-1, nx):
+                line = rxy[s, side(cy), side(cx)]
+            else:
+                line = ry[s, side(cy), j, at]
+            edge = jnp.broadcast_to(line, (ny, nz))
             value = jnp.where(first_row if cy == 1 else last_row, edge, value)
         if cz:
             j = MEMBERS[2, cz].index(q)
@@ -578,6 +580,8 @@
             pltpu.VMEM((STEPS, 2, FACE, nx + 2, 1, nz), f32),
             pltpu.VMEM((STEPS, 2, ny, nz), f32),
             pltpu.VMEM((STEPS, 2, ny, nz), f32),
+            pltpu.VMEM((STEPS, 2, 2, 1, nz), f32),
+            pltpu.VMEM((STEPS, 2, 2, 1, nz), f32),
             pltpu.VMEM((STEPS, 2, 2, 1, nz), f32),
             pltpu.VMEM((STEPS, 2, 2, 1, nz), f32),
             pltpu.VMEM((STEPS, 2, 2, 1, nz), f32),

time: 21.7 us -> 21.7 us (level)
  no operation moved by 1% of the time
where the time goes in v6:
time: 21.7 us; the launch traced here: 21.6 us
  Pallas kernels  20.9 us (96%)
  between operations  0.64 us (3%)
    pallas_call x1, Pallas kernels, per_device(): pl.pallas_call(functools.partial(kernel, sizes), out_shape=pltpu.VMEM((27...  20 us
    pallas_call x1, Pallas kernels, per_device(): pl.pallas_call(functools.partial(write_out, scale), out_shape=(jax.ShapeD...  0.91 us

profile of v6, /device:TPU:0, one launch (start us, length us, event | category | flops | bytes accessed | tf_op | source)
XLA Modules:
  0.0 21.6 jit_solution(7939899451610735149)
XLA Ops:
  0.6 20.0 %shard_map.49.result = f32[27,8,8,128]{3,2,1,0:T(8,128)S(1)} custom-call(f32[19,8,8,128]{3,2,1,0:T(8,128)} %flow_in.1, f32[7,8,8,128]{3,2,1,0:T(8,128)} %heat_in.1), custom_call_target="tpu_custom_call" | custom-call | tf_op jit(solution)/shard_map/pallas_call | solution.py:568
  20.6 0.9 %shard_map.50 = (f32[19,8,8,128]{3,2,1,0:T(8,128)}, f32[7,8,8,128]{3,2,1,0:T(8,128)}, f32[1,1]{1,0:T(1,128)}) custom-call(f32[27,8,8,128]{3,2,1,0:T(8,128)S(1)} %shard_map.49.result), custom_call_target="tpu_custom_call" | custom-call | tf_op jit(solution)/shard_map/pallas_call | solution.py:601
